TPU v7x, 16 devices: a 4x2x1 block of a 4x4x4 slice. The times are simulated.
16 devices in a mesh: dp: 4 (over y, z, core), tp: 4 (over x).
Axes of the slice: x: 4, y: 2, z: 1, core: 2. Of those that a mesh axis runs over, the one named last changes fastest.
The devices are a block of a 4x4x4 slice.
Arguments:
- x: bfloat16 [3072, 6144], P(('dp', 'tp')), parts along dimension 0
- dy: bfloat16 [3072, 6144], P(('dp', 'tp')), parts along dimension 0
- gate: bfloat16 [3072, 16384], P('dp', 'tp'), parts along dimension 0
- up: bfloat16 [3072, 16384], P('dp', 'tp'), parts along dimension 0
- w_gate: bfloat16 [6144, 16384], P(None, 'tp')
- w_up: bfloat16 [6144, 16384], P(None, 'tp')
- w_down: bfloat16 [16384, 6144], P('tp')
Outputs:
- output 1: bfloat16 [3072, 6144], P(('dp', 'tp')), parts along dimension 0
- output 2: bfloat16 [24576, 16384], P('dp', 'tp'), parts along dimension 0
- output 3: bfloat16 [24576, 16384], P('dp', 'tp'), parts along dimension 0
- output 4: bfloat16 [65536, 6144], P(('dp', 'tp')), parts along dimension 0
There are 4 independent parts. A program takes and returns all parts, laid end to end along the dimension named above; an argument that names none is the same for every part.
All inputs are finite; a program needn't handle non-finite values.
Results may differ from a plain program's by a relative error of at most 0.012.
Values are sent between devices in bfloat16 or wider.
A program may use at most 1.5 GiB of HBM per device.

v0:
```python
import jax
import jax.numpy as jnp


def act(gate, up):
    return jax.nn.silu(gate) * up


def solution(mesh):
    def step(x, dy, gate, up, w_gate, w_up, w_down):
        hidden, back = jax.vjp(act, gate.astype(jnp.float32), up.astype(jnp.float32))
        d_hidden = jnp.dot(dy, w_down.T, preferred_element_type=jnp.float32)
        d_gate, d_up = (g.astype(jnp.bfloat16) for g in back(d_hidden))
        dx = jnp.dot(d_gate, w_gate.T) + jnp.dot(d_up, w_up.T)
        groups = mesh.shape["dp"]

        def by_group(a, b):
            a, b = (t.reshape(groups, -1, t.shape[-1]) for t in (a, b))
            product = jnp.einsum("gta,gtb->gab", a, b, preferred_element_type=jnp.float32)
            return product.astype(jnp.bfloat16).reshape(-1, b.shape[-1])

        return dx, by_group(x, d_gate), by_group(x, d_up), by_group(hidden.astype(jnp.bfloat16), dy)

    return step
```

profile of v0, /device:TPU:112, one launch (start us, length us, event | category | flops | bytes accessed | tf_op | source)
XLA Modules:
  0.0 685.5 jit_solution(3572334169083005985)
XLA Ops:
  7.2 0.1 all-gather.9.cloned.1.call-start
  7.2 0.7 all-gather.9.cloned.1.call-update
  8.0 0.1 all-gather.11.cloned.1.call-start
  8.0 2.4 collective-permute-start
  10.5 1.6 collective-permute-start.1
  12.1 0.1 all-gather.11.cloned.1.call-update
  12.2 0.1 reduce-scatter.4.cloned.1.call-start
  12.2 1.2 dynamic-slice.27
  16.1 86.8 %collective-permute-done = bf16[1,1,192,6144]{3,2,1,0:T(8,128)(2,1)} collective-permute-done((bf16[1,1,192,6144]{3,2,1,0:T(8,128)(2,1)}, bf16[1,1,192,6144]{3,2,1,0:T(8,128)(2,1)}, u32[]{:S(2)}, u32[]{:S(2)}) %collective-permute-start) | collective-permute-done | bytes 2359328 | tf_op jit(solution)/gta,gtb->gab/dot_general | solution.py:19
  102.9 1.7 collective-permute-start.2
  104.6 68.7 %all-gather.9.cloned.1.call-done = bf16[768,6144]{1,0:T(8,128)(2,1)} async-done(((bf16[192,6144]{1,0:T(8,128)(2,1)}), bf16[768,6144]{1,0:T(8,128)(2,1)}) %all-gather.9.cloned.1.call-update) | async-done | bytes 9437200 | tf_op args[1]
  173.2 45.2 %fusion.24 = f32[768,4096]{1,0:T(8,128)S(1)} fusion(bf16[768,6144]{1,0:T(8,128)(2,1)} %all-gather.9.cloned.1.call-done, bf16[4096,6144]{1,0:T(8,128)(2,1)} %param.3), kind=kOutput, calls=%fused_computation.39 | convolution fusion | flops 38654705664 | bytes 72351744 | tf_op jit(solution)/dot_general | solution.py:12
  218.4 0.0 copy-start
  218.4 16.3 %fusion.8 = (bf16[1,1,768,4096]{3,2,1,0:T(8,128)(2,1)}, bf16[768,4096]{1,0:T(8,128)(2,1)}) fusion(bf16[768,4096]{1,0:T(8,128)(2,1)} %param.4, bf16[768,4096]{1,0:T(8,128)(2,1)} %param.5, f32[768,4096]{1,0:T(8,128)S(1)} %fusion.24), kind=kLoop, calls=%fused_computation.23 | loop fusion | flops 50331648 | bytes 37748736 | tf_op jit(solution)/gta,gtb->gab/dot_general | solution.py:19
  234.8 0.0 copy-done
  234.8 46.9 %fusion.25 = bf16[768,6144]{1,0:T(8,128)(2,1)} fusion(bf16[768,4096]{1,0:T(8,128)(2,1)} %get-tuple-element.17, bf16[6144,4096]{1,0:T(8,128)(2,1)} %param.6), kind=kOutput, calls=%fused_computation.40 | convolution fusion | flops 38654705664 | bytes 66060288 | tf_op jit(solution)/dot_general | solution.py:14
  281.7 65.8 %convolution_add_fusion = bf16[768,6144]{1,0:T(8,128)(2,1)} fusion(bf16[768,6144]{1,0:T(8,128)(2,1)} %fusion.25, bf16[6144,4096]{1,0:T(8,128)(2,1)} %param.7, f32[768,4096]{1,0:T(8,128)} %copy-done, bf16[768,4096]{1,0:T(8,128)(2,1)} %param.5), kind=kOutput, calls=%fused_computation.22 | convolution fusion | flops 38681444352 | bytes 88080384 | tf_op jit(solution)/dot_general | solution.py:14
  347.6 0.1 reduce-scatter.4.cloned.1.call-update
  347.6 0.0 all-gather.11.cloned.1.call-done
  347.6 47.6 %convert_bitcast_fusion.1 = bf16[6144,4096]{0,1:T(8,128)(2,1)} fusion(bf16[768,4096]{1,0:T(8,128)(2,1)} %get-tuple-element.17, bf16[768,6144]{1,0:T(8,128)(2,1)} %all-gather.11.cloned.1.call-done), kind=kOutput, calls=%fused_computation.3 | convolution fusion | flops 38679871488 | bytes 66060288 | tf_op jit(solution)/gta,gtb->gab/dot_general | solution.py:19
  395.2 64.5 %copy = bf16[6144,4096]{1,0:T(8,128)(2,1)} copy(bf16[6144,4096]{0,1:T(8,128)(2,1)} %convert_bitcast_fusion.1) | data formatting | bytes 100663296
  459.7 59.4 %convert_bitcast_fusion = bf16[6144,4096]{0,1:T(8,128)(2,1)} fusion(bf16[768,6144]{1,0:T(8,128)(2,1)} %all-gather.11.cloned.1.call-done, f32[768,4096]{1,0:T(8,128)} %copy-done, bf16[768,4096]{1,0:T(8,128)(2,1)} %param.5), kind=kOutput, calls=%fused_computation.2 | convolution fusion | flops 38701891584 | bytes 78643200 | tf_op jit(solution)/gta,gtb->gab/dot_general | solution.py:19
  519.1 0.0 copy-start.1
  519.1 64.7 %copy.1 = bf16[6144,4096]{1,0:T(8,128)(2,1)} copy(bf16[6144,4096]{0,1:T(8,128)(2,1)} %convert_bitcast_fusion) | data formatting | bytes 100663296
  583.8 0.0 copy-done.1
  583.8 40.5 %fusion.9 = f32[4096,6144,1]{1,0,2:T(8,128)} fusion(bf16[1,1,192,6144]{3,2,1,0:T(8,128)(2,1)} %collective-permute-done, bf16[1,1,192,6144]{3,2,1,0:T(8,128)(2,1)S(1)} %bitcast.61, s32[]{:T(128)} %bitcast.8, bf16[1,1,768,4096]{3,2,1,0:T(8,128)(2,1)} %get-tuple-element.16, s32[]{:T(128)} %bitcast.9), kind=kOutput, calls=%fused_computation.25 | convolution fusion | flops 19336003584 | bytes 111673352 | tf_op jit(solution)/gta,gtb->gab/dot_general | solution.py:19
  624.3 0.0 collective-permute-done.1
  624.3 0.0 collective-permute-done.2
  624.3 54.3 %fusion = bf16[4096,6144]{1,0:T(8,128)(2,1)} fusion(f32[4096,6144,1]{1,0,2:T(8,128)} %fusion.9, bf16[1,1,192,6144]{3,2,1,0:T(8,128)(2,1)} %collective-permute-done.2, bf16[1,1,192,6144]{3,2,1,0:T(8,128)(2,1)} %collective-permute-done.1, s32[]{:T(128)} %bitcast.14, bf16[1,1,768,4096]{3,2,1,0:T(8,128)(2,1)} %get-tuple-element.16, s32[]{:T(128)} %bitcast.15), kind=kOutput, calls=%fused_computation.1 | convolution fusion | flops 19386335232 | bytes 162004992 | tf_op jit(solution)/gta,gtb->gab/dot_general | solution.py:19
  678.7 0.0 reduce-scatter.4.cloned.1.call-done
Async XLA Ops:
  7.2 166.1 %all-gather.9.cloned.1.call-start = ((), (), s32[]{:S(2)}) async-start(), calls=%async_computation.1 | async-start | bytes 11796480 | tf_op args[1]
  8.0 339.7 %all-gather.11.cloned.1.call-start = ((), (), s32[]{:S(2)}) async-start(), calls=%async_computation.2 | async-start | bytes 11796480 | tf_op jit(solution)/reshape | solution.py:18
  8.0 94.8 %collective-permute-start = (bf16[1,1,192,6144]{3,2,1,0:T(8,128)(2,1)}, bf16[1,1,192,6144]{3,2,1,0:T(8,128)(2,1)}, u32[]{:S(2)}, u32[]{:S(2)}) collective-permute-start(bf16[1,1,192,6144]{3,2,1,0:T(8,128)(2,1)} %bitcast.59), channel_id=9, source_target_pairs={{0,1},{1,2},{2,3},{3,0},{4,5},{5,6},{6,7},{7,4},{8,9},{9,10},{10,1... | collective-permute-start | bytes 7077896 | tf_op jit(solution)/gta,gtb->gab/dot_general | solution.py:19
  10.5 613.9 %collective-permute-start.1 = (bf16[1,1,192,6144]{3,2,1,0:T(8,128)(2,1)}, bf16[1,1,192,6144]{3,2,1,0:T(8,128)(2,1)}, u32[]{:S(2)}, u32[]{:S(2)}) collective-permute-start(bf16[1,1,192,6144]{3,2,1,0:T(8,128)(2,1)} %bitcast.60), channel_id=10, source_target_pairs={{0,3},{1,0},{2,1},{3,2},{4,7},{5,4},{6,5},{7,6},{8,11},{9,8},{10,9... | collective-permute-start | bytes 7077896 | tf_op jit(solution)/gta,gtb->gab/dot_general | solution.py:19
  12.2 666.5 %reduce-scatter.4.cloned.1.call-start = ((), (), s32[]{:S(2)}) async-start(), calls=%async_computation.3 | async-start | bytes 11796480
  102.9 521.5 %collective-permute-start.2 = (bf16[1,1,192,6144]{3,2,1,0:T(8,128)(2,1)}, bf16[1,1,192,6144]{3,2,1,0:T(8,128)(2,1)}, u32[]{:S(2)}, u32[]{:S(2)}) collective-permute-start(bf16[1,1,192,6144]{3,2,1,0:T(8,128)(2,1)} %collective-permute-done), channel_id=11, source_target_pairs={{0,1},{1,2},{2,3},{3,0},{4,5},{5,6},{6,7},{7,4},{8,9},{9,10},{10,1... | collective-permute-start | bytes 7077896 | tf_op jit(solution)/gta,gtb->gab/dot_general | solution.py:19
  218.4 16.3 %copy-start = (f32[768,4096]{1,0:T(8,128)}, f32[768,4096]{1,0:T(8,128)S(1)}, u32[]{:S(2)}) copy-start(f32[768,4096]{1,0:T(8,128)S(1)} %fusion.24) | copy-start | bytes 37748740
  519.1 64.7 %copy-start.1 = (bf16[192,6144]{1,0:T(8,128)(2,1)S(1)}, bf16[192,6144]{1,0:T(8,128)(2,1)}, u32[]{:S(2)}) copy-start(bf16[192,6144]{1,0:T(8,128)(2,1)} %param.2) | copy-start | bytes 7077892
Sparse Core Ops, SparseCore 0:
  9.6 163.6 all-gather.8
  174.8 91.0 all-gather.10
  347.7 85.3 reduce-scatter.3
where the time goes:
time: 695 us; the launch traced here: 685 us
  matrix products  360 us (52%)
  waiting for transfers between devices  156 us (22%)
  local copies, waits for them, and re-layouts  130 us (19%)
  between operations  16.7 us (2%)
  other arithmetic  16.3 us (2%)
    dot_general x4, matrix products, by_group(): jnp.einsum('gta,gtb->gab', a, b, preferred_element_type=jnp.float32)  202 us
    unnamed x6, local copies, waits for them, and re-layouts  129 us
    dot_general x2, matrix products, step(): dx = jnp.dot(d_gate, w_gate.T) + jnp.dot(d_up, w_up.T)  113 us
    dot_general x3, waiting for transfers between devices, by_group(): jnp.einsum('gta,gtb->gab', a, b, preferred_element_type=jnp.float32)  86.8 us
    unnamed x5, waiting for transfers between devices  69.5 us
    dot_general x1, matrix products, step(): d_hidden = jnp.dot(dy, w_down.T, preferred_element_type=jnp.float32)  45.2 us
    dot_general x1, other arithmetic, by_group(): jnp.einsum('gta,gtb->gab', a, b, preferred_element_type=jnp.float32)  16.3 us
  transfers between devices with their start and end apart: 6, of which 2 were waited for; matrix products, arithmetic and copies ran while one was open for 74% of the time, Pallas kernels for 0%

commit v1 on v0

v1 whole, which is shorter than its diff:
```python
import functools

import jax
import jax.numpy as jnp
from jax import lax
from jax.experimental import pallas as pl
from jax.experimental.pallas import tpu as pltpu
from jax.sharding import PartitionSpec as P

MESH = pl.DeviceIdType.MESH
BF16, F32 = jnp.bfloat16, jnp.float32
VMEM_LIMIT = 66_000_000

CB = 512
FT = 2048
ET = 512
NT = 256
DT = 384


def dot_nt(a, b):
    return lax.dot_general(a, b, (((1,), (1,)), ((), ())), preferred_element_type=F32)


def dot_tn(a, b):
    return lax.dot_general(a, b, (((0,), (0,)), ((), ())), preferred_element_type=F32)


def ring(n):
    me = lax.axis_index("tp")
    return me, lax.rem(me + 1, n), lax.rem(me + n - 1, n), lax.rem(me + 2, n)


def greet(right, left):
    barrier = pltpu.get_barrier_semaphore()
    for other in (left, right):
        pl.semaphore_signal(barrier, inc=1, device_id={"tp": other}, device_id_type=MESH)
    pl.semaphore_wait(barrier, 2)


def rows_of(device, share, start, size):
    return pl.ds(pl.multiple_of(device * share + start, 16), size)


def remote(src, dst, send, recv, to):
    return pltpu.make_async_remote_copy(
        src_ref=src, dst_ref=dst, send_sem=send, recv_sem=recv, device_id={"tp": to}, device_id_type=MESH
    )


def first_kernel(n, dy, gate, up, wd, dg, du, dwd, dyf, hid_t, acc, wbuf, obuf, gu, eo, lsem, ssem, rsem, wsem, osem, gsem, esem):
    me, right, left, opposite = ring(n)
    share = dy.shape[0]
    half = share // 2
    blocks, _, cb = dyf.shape
    ft = wbuf.shape[1]
    et = gu.shape[-1]
    steps_f = wd.shape[0] // ft
    tiles_e = gate.shape[1] // et
    per_step = ft // et

    def load(j):
        return pltpu.make_async_copy(dy.at[:, pl.ds(pl.multiple_of(j * cb, cb), cb)], dyf.at[j, rows_of(me, share, 0, share), :], lsem.at[j])

    def hop(kind, j, sending):
        to = right if kind % 2 == 0 else left
        if kind < 2:
            start, size = 0, share
            whose = me if sending else (left if kind == 0 else right)
        else:
            start, size = (0 if kind == 2 else half), half
            whose = (left if kind == 2 else right) if sending else opposite
        part = dyf.at[j, rows_of(whose, share, start, size), :]
        return remote(part, part, ssem.at[kind, j], rsem.at[kind, j], to)

    def send_own(j):
        hop(0, j, True).start()
        hop(1, j, True).start()

    def pass_on(j):
        for kind in (0, 1):
            hop(kind, j, False).wait_recv()
        hop(2, j, True).start()
        hop(3, j, True).start()

    def gu_copies(e, slot):
        cols = pl.ds(pl.multiple_of(e * et, et), et)
        return [pltpu.make_async_copy(a.at[:, cols], gu.at[slot, k], gsem.at[slot, k]) for k, a in enumerate((gate, up))]

    def eo_copies(e, slot):
        cols = pl.ds(pl.multiple_of(e * et, et), et)
        return [pltpu.make_async_copy(eo.at[slot, k], a.at[:, cols], esem.at[slot, k]) for k, a in enumerate((dg, du))]

    def tile(ref, j, f):
        return ref.at[pl.ds(pl.multiple_of(f * ft, ft), ft), pl.ds(pl.multiple_of(j * cb, cb), cb)]

    def w_copy(s):
        return pltpu.make_async_copy(tile(wd, s // steps_f, lax.rem(s, steps_f)), wbuf.at[lax.rem(s, 2)], wsem.at[lax.rem(s, 2)])

    def o_copy(s):
        return pltpu.make_async_copy(obuf.at[lax.rem(s, 2)], tile(dwd, s // steps_f, lax.rem(s, steps_f)), osem.at[lax.rem(s, 2)])

    for j in range(blocks):
        load(j).start()
    for c in gu_copies(0, 0):
        c.start()
    w_copy(0).start()
    greet(right, left)
    for j in range(blocks):
        load(j).wait()
        if j < 2:
            send_own(j)

    def hidden_step(e, _):
        slot = lax.rem(e, 2)
        for c in gu_copies(e, slot):
            c.wait()

        @pl.when(e + 1 < tiles_e)
        def _():
            for c in gu_copies(e + 1, 1 - slot):
                c.start()

        g = gu[slot, 0].astype(F32)
        u = gu[slot, 1].astype(F32)
        hidden = (g * jax.nn.sigmoid(g) * u).astype(BF16)
        hid_t[pl.ds(pl.multiple_of(e * et, et), et), :] = hidden.T
        acc[e] = jnp.zeros(acc.shape[1:], F32)
        return 0

    lax.fori_loop(0, tiles_e // 2, hidden_step, 0)
    pass_on(0)
    send_own(2)
    lax.fori_loop(tiles_e // 2, tiles_e, hidden_step, 0)

    total = blocks * steps_f

    def step(s, _):
        j = s // steps_f
        f = lax.rem(s, steps_f)
        slot = lax.rem(s, 2)

        @pl.when(f == 0)
        def _():
            for kind in (2, 3):
                hop(kind, j, False).wait_recv()

            @pl.when(j + 1 < blocks)
            def _():
                pass_on(j + 1)

            @pl.when(j + 3 < blocks)
            def _():
                send_own(j + 3)

        w_copy(s).wait()

        @pl.when(s + 1 < total)
        def _():
            w_copy(s + 1).start()

        @pl.when(s >= 2)
        def _():
            o_copy(s - 2).wait()

        block = dyf[j]
        for q in range(per_step):
            acc[f * per_step + q] += dot_nt(block, wbuf[slot, q * et : (q + 1) * et, :])
        obuf[slot] = jnp.dot(hid_t[pl.ds(pl.multiple_of(f * ft, ft), ft), :], block, preferred_element_type=F32).astype(BF16)
        o_copy(s).start()
        return 0

    for c in gu_copies(0, 0):
        c.start()
    lax.fori_loop(0, total, step, 0)

    def grad_step(e, _):
        slot = lax.rem(e, 2)
        for c in gu_copies(e, slot):
            c.wait()

        @pl.when(e + 1 < tiles_e)
        def _():
            for c in gu_copies(e + 1, 1 - slot):
                c.start()

        @pl.when(e >= 2)
        def _():
            for c in eo_copies(e - 2, slot):
                c.wait()

        g = gu[slot, 0].astype(F32)
        u = gu[slot, 1].astype(F32)
        d = acc[e]
        sig = jax.nn.sigmoid(g)
        silu = g * sig
        eo[slot, 0] = (d * u * (sig + silu * (1.0 - sig))).astype(BF16)
        eo[slot, 1] = (d * silu).astype(BF16)
        for c in eo_copies(e, slot):
            c.start()
        return 0

    lax.fori_loop(0, tiles_e, grad_step, 0)
    for s in (total - 2, total - 1):
        o_copy(s).wait()
    for e in (tiles_e - 2, tiles_e - 1):
        for c in eo_copies(e, e % 2):
            c.wait()
    for j in range(blocks):
        for kind in range(4):
            hop(kind, j, True).wait_send()


def second_kernel(n, dg, du, wg, wu, x, s1r, s1l, s2r, s2l, accr, accl, own, xf, res, lsem, ssem, rsem):
    i = pl.program_id(0)
    steps = pl.num_programs(0)
    me, right, left, opposite = ring(n)
    share = x.shape[0]
    half = share // 2
    quarter = half // 2

    def hop(kind, part, sending):
        to = right if kind % 2 == 0 else left
        if kind < 2:
            whose = me if sending else (left if kind == 0 else right)
        else:
            whose = (left if kind == 2 else right) if sending else opposite
        dst = xf.at[rows_of(whose, share, part * half, half), :]
        src = x.at[pl.ds(part * half, half), :] if sending and kind < 2 else dst
        sem = 2 * kind + part
        return remote(src, dst, ssem.at[sem], rsem.at[sem], to)

    local = pltpu.make_async_copy(x, xf.at[rows_of(me, share, 0, share), :], lsem)

    @pl.when(i == 0)
    def _():
        local.start()
        greet(right, left)
        hop(0, 0, True).start()
        hop(1, 1, True).start()
        hop(0, 1, True).start()
        hop(1, 0, True).start()

    @pl.when(i == steps * 3 // 8)
    def _():
        hop(0, 0, False).wait_recv()
        hop(2, 0, True).start()
        hop(1, 1, False).wait_recv()
        hop(3, 1, True).start()

    res[...] = dot_nt(dg[...], wg[...]) + dot_nt(du[...], wu[...])

    def term(device, start, size):
        return res[rows_of(device, share, start, size), :]

    s1r[:half, :] = term(opposite, 0, half).astype(BF16)
    s1r[half:, :] = term(right, half, quarter).astype(BF16)
    s2r[...] = term(right, half + quarter, quarter).astype(BF16)
    accr[...] = term(right, 0, half)
    s1l[:half, :] = term(opposite, half, half).astype(BF16)
    s1l[half:, :] = term(left, 0, quarter).astype(BF16)
    s2l[...] = term(left, quarter, quarter).astype(BF16)
    accl[...] = term(left, half, half)
    own[...] = term(me, 0, share)

    @pl.when(i == steps - 1)
    def _():
        local.wait()
        hop(0, 1, False).wait_recv()
        hop(1, 0, False).wait_recv()
        hop(2, 0, False).wait_recv()
        hop(3, 1, False).wait_recv()
        for kind, part in ((0, 0), (0, 1), (1, 0), (1, 1), (2, 0), (3, 1)):
            hop(kind, part, True).wait_send()


def gate_kernel(xf, g, out):
    out[...] = dot_tn(xf[...], g[...]).astype(BF16)


def up_kernel(xf, g, ready, out, copied):
    out[...] = dot_tn(xf[...], g[...]).astype(BF16)
    copied[...] = ready[...]


def cost(flops, nbytes):
    return pl.CostEstimate(flops=flops, bytes_accessed=nbytes, transcendentals=0)


def solution(mesh):
    n = mesh.shape["tp"]

    def body(x, dy, gate, up, w_gate, w_up, w_down):
        share, width = x.shape
        rows, ff = gate.shape
        blocks = width // CB
        any_, vmem = pl.BlockSpec(memory_space=pl.ANY), pltpu.VMEM
        flops = 2 * rows * width * ff
        act, wbytes = rows * ff * 2, width * ff * 2
        one = pl.Buffered(1)

        dg, du, dwd = pl.pallas_call(
            functools.partial(first_kernel, n),
            out_shape=[jax.ShapeDtypeStruct((rows, ff), BF16)] * 2 + [jax.ShapeDtypeStruct((ff, width), BF16)],
            in_specs=[any_] * 4,
            out_specs=[any_] * 3,
            scratch_shapes=[
                vmem((blocks, rows, CB), BF16),
                vmem((ff, rows), BF16),
                vmem((ff // ET, rows, ET), F32),
                vmem((2, FT, CB), BF16),
                vmem((2, FT, CB), BF16),
                vmem((2, 2, rows, ET), BF16),
                vmem((2, 2, rows, ET), BF16),
                pltpu.SemaphoreType.DMA((blocks,)),
                pltpu.SemaphoreType.DMA((4, blocks)),
                pltpu.SemaphoreType.DMA((4, blocks)),
                pltpu.SemaphoreType.DMA((2,)),
                pltpu.SemaphoreType.DMA((2,)),
                pltpu.SemaphoreType.DMA((2, 2)),
                pltpu.SemaphoreType.DMA((2, 2)),
            ],
            compiler_params=pltpu.CompilerParams(collective_id=0, has_side_effects=True, vmem_limit_bytes=VMEM_LIMIT),
            cost_estimate=cost(2 * flops, 2 * wbytes + 6 * act),
            name="dhidden_dwdown",
        )(dy, gate, up, w_down)

        half, quarter = share // 2, share // 4

        def strip(count, dtype):
            return jax.ShapeDtypeStruct((count, width), dtype), pl.BlockSpec((count, NT), lambda i: (0, i))

        strips = [strip(half + quarter, BF16)] * 2 + [strip(quarter, BF16)] * 2 + [strip(half, F32)] * 2 + [strip(share, F32)]
        whole = pl.BlockSpec((rows, ff), lambda i: (0, 0), pipeline_mode=one)
        s1r, s1l, s2r, s2l, accr, accl, own, xf = pl.pallas_call(
            functools.partial(second_kernel, n),
            grid=(width // NT,),
            out_shape=[a for a, _ in strips] + [jax.ShapeDtypeStruct((rows, width), BF16)],
            in_specs=[whole, whole, pl.BlockSpec((NT, ff), lambda i: (i, 0)), pl.BlockSpec((NT, ff), lambda i: (i, 0)), any_],
            out_specs=[b for _, b in strips] + [any_],
            scratch_shapes=[
                vmem((rows, NT), F32),
                pltpu.SemaphoreType.DMA,
                pltpu.SemaphoreType.DMA((8,)),
                pltpu.SemaphoreType.DMA((8,)),
            ],
            compiler_params=pltpu.CompilerParams(
                collective_id=1, has_side_effects=True, vmem_limit_bytes=VMEM_LIMIT, dimension_semantics=("arbitrary",)
            ),
            cost_estimate=cost(2 * flops, 2 * wbytes + 6 * act),
            name="dx_gather",
        )(dg, du, w_gate, w_up, x)

        to_right = [(i, (i + 1) % n) for i in range(n)]
        to_left = [(i, (i - 1) % n) for i in range(n)]
        r1r = lax.ppermute(s1r, "tp", to_right)
        r1l = lax.ppermute(s1l, "tp", to_left)

        x_spec = pl.BlockSpec((rows, DT), lambda i: (0, i))
        out_spec = pl.BlockSpec((DT, ff), lambda i: (i, 0))
        plain = pltpu.CompilerParams(vmem_limit_bytes=VMEM_LIMIT, dimension_semantics=("arbitrary",))
        dwg = pl.pallas_call(
            gate_kernel,
            grid=(width // DT,),
            out_shape=jax.ShapeDtypeStruct((width, ff), BF16),
            in_specs=[x_spec, whole],
            out_specs=out_spec,
            compiler_params=plain,
            cost_estimate=cost(flops, wbytes + 3 * act),
            name="dw_gate",
        )(xf, dg)

        s2r = jnp.concatenate([(accr + r1r[:half].astype(F32)).astype(BF16), s2r])
        s2l = jnp.concatenate([(accl + r1l[:half].astype(F32)).astype(BF16), s2l])
        r2r = lax.ppermute(s2r, "tp", to_right)
        r2l = lax.ppermute(s2l, "tp", to_left)

        copy_spec = pl.BlockSpec((ff * DT // width, width), lambda i: (i, 0))
        dwu, dwd = pl.pallas_call(
            up_kernel,
            grid=(width // DT,),
            out_shape=[jax.ShapeDtypeStruct((width, ff), BF16), jax.ShapeDtypeStruct((ff, width), BF16)],
            in_specs=[x_spec, whole, copy_spec],
            out_specs=[out_spec, copy_spec],
            compiler_params=plain,
            cost_estimate=cost(flops, 3 * wbytes + 3 * act),
            name="dw_up",
        )(xf, du, dwd)

        f32 = lambda a: a.astype(F32)
        first = f32(jnp.concatenate([r2r[:half], r2l[:half]]))
        second = f32(jnp.concatenate([r1l[half:], r2l[half:], r1r[half:], r2r[half:]]))
        return (own + first + second).astype(BF16), dwg, dwu, dwd

    part, cols = P(("dp", "tp"), None), P("dp", "tp")
    return jax.shard_map(
        body,
        mesh=mesh,
        in_specs=(part, part, cols, cols, P(None, "tp"), P(None, "tp"), P("tp", None)),
        out_specs=(part, cols, cols, part),
        check_vma=False,
    )
```

time: 695 us -> 350 us (0.50); the launches traced: 685 us -> 349 us
  matrix products: 360 us -> 0 us
  Pallas kernels: 0 us -> 324 us
  waiting for transfers between devices: 156 us -> 0.01 us
  local copies, waits for them, and re-layouts: 130 us -> 7.97 us
  between operations: 16.7 us -> 0.74 us
    dot_general x7 -> x0, matrix products: 360 us -> none  [the longest x4 202 us: by_group(): jnp.einsum('gta,gtb->gab', a, b, preferred_element_type=jnp.float32)]
    pallas_call x0 -> x4, Pallas kernels: none -> 324 us  [the longest x1 115 us: body(): pl.pallas_call(functools.partial(first_kernel, n), out_shape=[jax.ShapeDt...]
    unnamed x6, local copies, waits for them, and re-layouts: 129 us -> 0.86 us
    dot_general x3 -> x0, waiting for transfers between devices: 86.8 us -> none  [by_group(): jnp.einsum('gta,gtb->gab', a, b, preferred_element_type=jnp.float32)]
    unnamed x5 -> x0, waiting for transfers between devices: 69.5 us -> none
    dot_general x1 -> x0, other arithmetic: 16.3 us -> none  [by_group(): jnp.einsum('gta,gtb->gab', a, b, preferred_element_type=jnp.float32)]
    convert_element_type x0 -> x3, other arithmetic: none -> 7.77 us  [the longest x1 3.9 us: body(): return ((own + first + second).astype(BF16), dwg, dwu, dwd)]
    slice x0 -> x6, local copies, waits for them, and re-layouts: none -> 7.11 us  [the longest x2 2.7 us: body(): first = f32(jnp.concatenate([r2r[:half], r2l[:half]]))]
  transfers between devices with their start and end apart: 6 -> 4, of which waited for: 2 -> 0; matrix products, arithmetic and copies ran while one was open for 74% -> 3% of each run, Pallas kernels for 0% -> 32%
where the time goes in v1:
time: 350 us; the launch traced here: 349 us
  Pallas kernels  324 us (93%)
  other arithmetic  10.5 us (3%)
  local copies, waits for them, and re-layouts  7.97 us (2%)
  starting transfers between devices  5.69 us (2%)
    pallas_call x1, Pallas kernels, body(): pl.pallas_call(functools.partial(first_kernel, n), out_shape=[jax.ShapeDt...  115 us
    pallas_call x1, Pallas kernels, body(): pl.pallas_call(functools.partial(second_kernel, n), grid=(width // NT,),...  95.9 us
    pallas_call x1, Pallas kernels, body(): pl.pallas_call(up_kernel, grid=(width // DT,), out_shape=[jax.ShapeDtypeS...  65.9 us
    pallas_call x1, Pallas kernels, body(): pl.pallas_call(gate_kernel, grid=(width // DT,), out_shape=jax.ShapeDtype...  47 us
  transfers between devices with their start and end apart: 4, of which 0 were waited for; matrix products, arithmetic and copies ran while one was open for 3% of the time, Pallas kernels for 32%

profile of v1, /device:TPU:112, one launch (start us, length us, event | category | flops | bytes accessed | tf_op | source)
XLA Modules:
  0.0 349.1 jit_solution(15128651536249286875)
XLA Ops:
  0.6 115.3 %dhidden_dwdown.1 = (bf16[768,4096]{1,0:T(8,128)(2,1)}, bf16[768,4096]{1,0:T(8,128)(2,1)}, bf16[4096,6144]{1,0:T(8,128)(2,1)}) custom-call(bf16[192,6144]{1,0:T(8,128)(2,1)} %dy.1, bf16[768,4096]{1,0:T(8,128)(2,1)} %gate.1, bf16[768,4096]{1,0:T(8,128)(2,1)} %up.1, bf16[4096,6144]{1,0:T(8,128)(2,1)} %wd.1), custom_call_target="tpu_custom_call" | custom-call | flops 77309411328 | bytes 138412032 | tf_op jit(solution)/shard_map/dhidden_dwdown/pallas_call | solution.py:302
  115.9 95.9 %dx_gather.1 = (bf16[144,6144]{1,0:T(8,128)(2,1)}, bf16[144,6144]{1,0:T(8,128)(2,1)}, bf16[48,6144]{1,0:T(8,128)(2,1)}, bf16[48,6144]{1,0:T(8,128)(2,1)}, f32[96...) custom-call(bf16[768,4096]{1,0:T(8,128)(2,1)} %get-tuple-element.17.dg.g, ...), custom_call_target="tpu_custom_call" | custom-call | flops 77309411328 | bytes 138412032 | tf_op jit(solution)/shard_map/dx_gather/pallas_call | solution.py:335
  211.8 0.1 collective-permute-start
  211.9 3.2 collective-permute-start.2
  215.1 47.0 %dw_gate.1 = bf16[6144,4096]{1,0:T(8,128)(2,1)} custom-call(bf16[768,6144]{1,0:T(8,128)(2,1)} %get-tuple-element.26.xf, bf16[768,4096]{1,0:T(8,128)(2,1)} %get-tuple-element.17.dg.g), custom_call_target="tpu_custom_call" | custom-call | flops 38654705664 | bytes 69206016 | tf_op jit(solution)/shard_map/dw_gate/pallas_call | solution.py:362
  262.2 0.0 collective-permute-done
  262.2 0.0 copy-start.2
  262.2 2.3 add_convert_fusion.2
  264.5 0.0 copy-start
  264.5 0.0 copy-done.2
  264.5 1.4 pad_maximum_fusion
  265.9 0.0 collective-permute-start.1
  265.9 0.0 collective-permute-done.2
  265.9 0.9 copy-done
  266.8 0.0 copy-start.1
  266.8 1.6 add_convert_fusion.1
  268.4 0.0 copy-done.1
  268.4 1.3 pad_maximum_fusion.1
  269.7 2.4 collective-permute-start.3
  272.1 65.9 %dw_up.1 = (bf16[6144,4096]{1,0:T(8,128)(2,1)}, bf16[4096,6144]{1,0:T(8,128)(2,1)}) custom-call(bf16[768,6144]{1,0:T(8,128)(2,1)} %get-tuple-element.26.xf, bf16[768,4096]{1,0:T(8,128)(2,1)} %get-tuple-element.18.du.g, bf16[4096,6144]{1,0:T(8,128)(2,1)} %get-tuple-element.27.ready), custom_call_target="tpu_custom_call" | custom-call | flops 38654705664 | bytes 169869312 | tf_op jit(solution)/shard_map/dw_up/pallas_call | solution.py:379
  338.0 1.1 slice.36
  339.1 1.1 slice.38
  340.3 0.0 collective-permute-done.1
  340.3 1.3 slice.33
  341.6 1.1 slice.39
  342.7 0.0 collective-permute-done.3
  342.7 1.3 slice.35
  344.1 1.1 slice.37
  345.2 3.9 %add_convert_fusion = bf16[192,6144]{1,0:T(8,128)(2,1)} fusion(f32[192,6144]{1,0:T(8,128)} %get-tuple-element.19, bf16[96,6144]{1,0:T(8,128)(2,1)S(1)} %slice.35, bf16[96,6144]{1,0:T(8,128)(2,1)S(1)} %slice.33, bf16[48,6144]{1,0:T(8,128)(2,1)S(1)} %slice.39, bf16[48,6144]{1,0:T(8,128)(2,1)S(1)} %slice.38, bf16[48,6144]{1,0:T(8,128)(2,1)S(1)} %slice.37, ...), kind=kLoop, calls=%fused_computation | loop fusion | flops 17694720 | bytes 11796480 | tf_op jit(solution)/shard_map/convert_element_type | solution.py:393
Async XLA Ops:
  211.8 50.4 %collective-permute-start = (bf16[144,6144]{1,0:T(8,128)(2,1)}, bf16[144,6144]{1,0:T(8,128)(2,1)}, u32[]{:S(2)}, u32[]{:S(2)}) collective-permute-start(bf16[144,6144]{1,0:T(8,128)(2,1)} %get-tuple-element.21), channel_id=1, source_target_pairs={{0,1},{1,2},{2,3},{3,0},{4,5},{5,6},{6,7},{7,4},{8,9},{9,10},{10,1... | collective-permute-start | bytes 5308424 | tf_op jit(solution)/shard_map/ppermute | solution.py:356
  211.9 54.0 %collective-permute-start.2 = (bf16[144,6144]{1,0:T(8,128)(2,1)}, bf16[144,6144]{1,0:T(8,128)(2,1)}, u32[]{:S(2)}, u32[]{:S(2)}) collective-permute-start(bf16[144,6144]{1,0:T(8,128)(2,1)} %get-tuple-element.24), channel_id=1, source_target_pairs={{0,3},{1,0},{2,1},{3,2},{4,7},{5,4},{6,5},{7,6},{8,11},{9,8},{10,9... | collective-permute-start | bytes 5308424 | tf_op jit(solution)/shard_map/ppermute | solution.py:357
  262.2 2.3 copy-start.2
  264.5 2.3 copy-start
  265.9 74.4 %collective-permute-start.1 = (bf16[144,6144]{1,0:T(8,128)(2,1)}, bf16[144,6144]{1,0:T(8,128)(2,1)}, u32[]{:S(2)}, u32[]{:S(2)}) collective-permute-start(bf16[144,6144]{1,0:T(8,128)(2,1)} %pad_maximum_fusion), channel_id=1, source_target_pairs={{0,1},{1,2},{2,3},{3,0},{4,5},{5,6},{6,7},{7,4},{8,9},{9,10},{10,1... | collective-permute-start | bytes 5308424 | tf_op jit(solution)/shard_map/ppermute | solution.py:375
  266.8 1.6 copy-start.1
  269.7 73.0 %collective-permute-start.3 = (bf16[144,6144]{1,0:T(8,128)(2,1)}, bf16[144,6144]{1,0:T(8,128)(2,1)}, u32[]{:S(2)}, u32[]{:S(2)}) collective-permute-start(bf16[144,6144]{1,0:T(8,128)(2,1)} %pad_maximum_fusion.1), channel_id=1, source_target_pairs={{0,3},{1,0},{2,1},{3,2},{4,7},{5,4},{6,5},{7,6},{8,11},{9,8},{10,9... | collective-permute-start | bytes 5308424 | tf_op jit(solution)/shard_map/ppermute | solution.py:376

commit v2 on v1

v2 whole, which is shorter than its diff:
```python
import functools

import jax
import jax.numpy as jnp
from jax import lax
from jax.experimental import pallas as pl
from jax.experimental.pallas import tpu as pltpu
from jax.sharding import PartitionSpec as P

MESH = pl.DeviceIdType.MESH
BF16, F32 = jnp.bfloat16, jnp.float32
VMEM_LIMIT = 66_000_000

CB = 512
FT = 1024
ET = 512
NT = 256
DT = 384
XR = 16
DELAY = 4
KEEP = DELAY + 2
SENDS = 4


def dot_nt(a, b):
    return lax.dot_general(a, b, (((1,), (1,)), ((), ())), preferred_element_type=F32)


def dot_tn(a, b):
    return lax.dot_general(a, b, (((0,), (0,)), ((), ())), preferred_element_type=F32)


def ring(n):
    me = lax.axis_index("tp")
    return me, lax.rem(me + 1, n), lax.rem(me + n - 1, n), lax.rem(me + 2, n)


def greet(right, left):
    barrier = pltpu.get_barrier_semaphore()
    for other in (left, right):
        pl.semaphore_signal(barrier, inc=1, device_id={"tp": other}, device_id_type=MESH)
    pl.semaphore_wait(barrier, 2)


def rows_of(device, share, start, size):
    return pl.ds(pl.multiple_of(device * share + start, 16), size)


def remote(src, dst, send, recv, to):
    return pltpu.make_async_remote_copy(
        src_ref=src, dst_ref=dst, send_sem=send, recv_sem=recv, device_id={"tp": to}, device_id_type=MESH
    )


def main_kernel(
    n,
    dy, gate, up, wd, wg, wu, x,
    dg, du, dwd, xf, to_r, to_l, own,
    dyf, hid_t, acc, dgv, duv, wbuf, obuf, gu, w2, rsend, rrecv,
    lsem, ssem, rsem, wsem, osem, gsem, dsem, w2sem, xsend, xrecv, ts, tr, s2sem, owsem,
):
    me, right, left, opposite = ring(n)
    share = dy.shape[0]
    half = share // 2
    blocks, _, cb = dyf.shape
    ft = wbuf.shape[1]
    et = gu.shape[-1]
    steps_f = wd.shape[0] // ft
    tiles_e = gate.shape[1] // et
    per_step = ft // et

    def load(j):
        return pltpu.make_async_copy(dy.at[:, pl.ds(pl.multiple_of(j * cb, cb), cb)], dyf.at[j, rows_of(me, share, 0, share), :], lsem.at[j])

    def hop(kind, j, sending):
        to = right if kind % 2 == 0 else left
        if kind < 2:
            start, size = 0, share
            whose = me if sending else (left if kind == 0 else right)
        else:
            start, size = (0 if kind == 2 else half), half
            whose = (left if kind == 2 else right) if sending else opposite
        part = dyf.at[j, rows_of(whose, share, start, size), :]
        return remote(part, part, ssem.at[kind, j], rsem.at[kind, j], to)

    def send_own(j):
        hop(0, j, True).start()
        hop(1, j, True).start()

    def pass_on(j):
        for kind in (0, 1):
            hop(kind, j, False).wait_recv()
        hop(2, j, True).start()
        hop(3, j, True).start()

    def gu_copies(e, slot):
        cols = pl.ds(pl.multiple_of(e * et, et), et)
        return [pltpu.make_async_copy(a.at[:, cols], gu.at[slot, k], gsem.at[slot, k]) for k, a in enumerate((gate, up))]

    def tile(ref, j, f):
        return ref.at[pl.ds(pl.multiple_of(f * ft, ft), ft), pl.ds(pl.multiple_of(j * cb, cb), cb)]

    def w_copy(s):
        return pltpu.make_async_copy(tile(wd, s // steps_f, lax.rem(s, steps_f)), wbuf.at[lax.rem(s, 2)], wsem.at[lax.rem(s, 2)])

    def o_copy(s):
        return pltpu.make_async_copy(obuf.at[lax.rem(s, 2)], tile(dwd, s // steps_f, lax.rem(s, steps_f)), osem.at[lax.rem(s, 2)])

    chunks = share // XR

    def xhop(kind, c, sending):
        to = right if kind % 2 == 0 else left
        if kind < 2:
            whose = me if sending else (left if kind == 0 else right)
        else:
            whose = (left if kind == 2 else right) if sending else opposite
        dst = xf.at[rows_of(whose, share, c * XR, XR), :]
        src = x.at[pl.ds(pl.multiple_of(c * XR, XR), XR), :] if sending and kind < 2 else dst
        return remote(src, dst, xsend.at[kind, c], xrecv.at[kind, c], to)

    def x_own(k):
        xhop(0, k, True).start()
        xhop(1, lax.rem(k + chunks // 2, chunks), True).start()

    def x_pass(k):
        xhop(0, k, False).wait_recv()
        xhop(2, k, True).start()
        xhop(1, k + chunks // 2, False).wait_recv()
        xhop(3, k + chunks // 2, True).start()

    x_local = pltpu.make_async_copy(x, xf.at[rows_of(me, share, 0, share), :], dsem.at[2])
    x_local.start()
    for j in range(blocks):
        load(j).start()
    for c in gu_copies(0, 0):
        c.start()
    w_copy(0).start()
    greet(right, left)
    for j in range(blocks):
        load(j).wait()
        if j < 2:
            send_own(j)

    def hidden_step(e, _):
        slot = lax.rem(e, 2)
        for c in gu_copies(e, slot):
            c.wait()

        @pl.when(e + 1 < tiles_e)
        def _():
            for c in gu_copies(e + 1, 1 - slot):
                c.start()

        g = gu[slot, 0].astype(F32)
        u = gu[slot, 1].astype(F32)
        hidden = (g * jax.nn.sigmoid(g) * u).astype(BF16)
        hid_t[pl.ds(pl.multiple_of(e * et, et), et), :] = hidden.T
        acc[e] = jnp.zeros(acc.shape[1:], F32)
        return 0

    lax.fori_loop(0, tiles_e // 2, hidden_step, 0)
    pass_on(0)
    send_own(2)
    lax.fori_loop(tiles_e // 2, tiles_e, hidden_step, 0)

    total = blocks * steps_f

    def step(s, _):
        j = s // steps_f
        f = lax.rem(s, steps_f)
        slot = lax.rem(s, 2)

        @pl.when(f == 0)
        def _():
            for kind in (2, 3):
                hop(kind, j, False).wait_recv()

            @pl.when(j + 1 < blocks)
            def _():
                pass_on(j + 1)

            @pl.when(j + 3 < blocks)
            def _():
                send_own(j + 3)

            @pl.when(j + 3 >= blocks)
            def _():
                x_own(j + 3 - blocks)

        w_copy(s).wait()

        @pl.when(s + 1 < total)
        def _():
            w_copy(s + 1).start()

        @pl.when(s >= 2)
        def _():
            o_copy(s - 2).wait()

        block = dyf[j]
        for q in range(per_step):
            acc[f * per_step + q] += dot_nt(block, wbuf[slot, q * et : (q + 1) * et, :])
        obuf[slot] = jnp.dot(hid_t[pl.ds(pl.multiple_of(f * ft, ft), ft), :], block, preferred_element_type=F32).astype(BF16)
        o_copy(s).start()
        return 0

    for c in gu_copies(0, 0):
        c.start()
    lax.fori_loop(0, total, step, 0)

    width = wg.shape[0]
    nt = w2.shape[2]
    tiles = width // nt
    res = acc.at[0, :, :nt]

    def keep(hold, k):
        return acc.at[1 + hold, k * half : (k + 1) * half, :nt]

    def sto(slot):
        return acc.at[1 + KEEP, pl.ds(pl.multiple_of(slot * share, 16), share), :nt]

    def st2(hold, k, start, size):
        return gu.at[hold // 4, k, pl.ds(pl.multiple_of(lax.rem(hold, 4) * share + start, 16), size), :nt]

    def w2_copies(t):
        slot = lax.rem(t, 2)
        part = pl.ds(pl.multiple_of(t * nt, nt), nt)
        return [pltpu.make_async_copy(a.at[part, :], w2.at[slot, k], w2sem.at[slot, k]) for k, a in enumerate((wg, wu))]

    for c in w2_copies(0):
        c.start()
    x_own(3)

    def grad_step(e, _):
        slot = lax.rem(e, 2)
        for c in gu_copies(e, slot):
            c.wait()

        @pl.when(e + 1 < tiles_e)
        def _():
            for c in gu_copies(e + 1, 1 - slot):
                c.start()

        @pl.when(lax.rem(e, 4) == 2)
        def _():
            x_own(4 + e // 4)

        g = gu[slot, 0].astype(F32)
        u = gu[slot, 1].astype(F32)
        d = acc[e]
        sig = jax.nn.sigmoid(g)
        silu = g * sig
        cols = pl.ds(pl.multiple_of(e * et, et), et)
        dgv[:, cols] = (d * u * (sig + silu * (1.0 - sig))).astype(BF16)
        duv[:, cols] = (d * silu).astype(BF16)
        return 0

    lax.fori_loop(0, tiles_e, grad_step, 0)
    d_copies = [pltpu.make_async_copy(v, o, dsem.at[k]) for k, (v, o) in enumerate(((dgv, dg), (duv, du)))]
    for c in d_copies:
        c.start()

    def t_hop(t, k, sending):
        slot = lax.rem(t, SENDS)
        return remote(rsend.at[slot, k], rrecv.at[t, k], ts.at[slot, k], tr.at[t, k], right if k == 0 else left)

    def s2_copies(t):
        slot = lax.rem(t, KEEP)
        part = pl.ds(pl.multiple_of(t * nt, nt), nt)
        return [pltpu.make_async_copy(st2(slot, k, 0, share), a.at[:, part], s2sem.at[slot, k]) for k, a in enumerate((to_r, to_l))]

    def own_copy(t):
        slot = lax.rem(t, 2)
        return pltpu.make_async_copy(sto(slot), own.at[:, pl.ds(pl.multiple_of(t * nt, nt), nt)], owsem.at[slot])

    def dx_step(t, _):
        @pl.when(jnp.logical_and(t >= 1, t <= tiles))
        def _():
            for k in (0, 1):
                t_hop(t - 1, k, True).start()

        @pl.when(jnp.logical_and(lax.rem(t, 4) == 0, t < 2 * chunks))
        def _():
            x_pass(t // 4)

        @pl.when(jnp.logical_and(lax.rem(t, 4) == 2, t < 2 * chunks))
        def _():
            x_own(chunks // 2 + t // 4)

        @pl.when(t < tiles)
        def _():
            slot = lax.rem(t, 2)
            for c in w2_copies(t):
                c.wait()

            @pl.when(t + 1 < tiles)
            def _():
                for c in w2_copies(t + 1):
                    c.start()

            @pl.when(t >= SENDS)
            def _():
                for k in (0, 1):
                    t_hop(t - SENDS, k, True).wait_send()

            @pl.when(t >= KEEP)
            def _():
                for c in s2_copies(t - KEEP):
                    c.wait()

            @pl.when(t >= 2)
            def _():
                own_copy(t - 2).wait()

            res[...] = dot_nt(dgv[...], w2[slot, 0]) + dot_nt(duv[...], w2[slot, 1])

            def term(device, start, size):
                return res[rows_of(device, share, start, size), :]

            hold = lax.rem(t, KEEP)
            out = lax.rem(t, SENDS)
            rsend[out, 0] = term(opposite, 0, half).astype(BF16)
            rsend[out, 1] = term(opposite, half, half).astype(BF16)
            keep(hold, 0)[...] = term(right, 0, half)
            keep(hold, 1)[...] = term(left, half, half)
            st2(hold, 0, half, half)[...] = term(right, half, half).astype(BF16)
            st2(hold, 1, 0, half)[...] = term(left, 0, half).astype(BF16)
            sto(slot)[...] = term(me, 0, share)
            own_copy(t).start()

        @pl.when(t >= DELAY)
        def _():
            u = t - DELAY
            hold = lax.rem(u, KEEP)
            for k in (0, 1):
                t_hop(u, k, False).wait_recv()
            st2(hold, 0, 0, half)[...] = (keep(hold, 0)[...] + rrecv[u, 0].astype(F32)).astype(BF16)
            st2(hold, 1, half, half)[...] = (keep(hold, 1)[...] + rrecv[u, 1].astype(F32)).astype(BF16)
            for c in s2_copies(u):
                c.start()

        return 0

    lax.fori_loop(0, tiles + DELAY, dx_step, 0)

    for s in (total - 2, total - 1):
        o_copy(s).wait()
    for c in d_copies:
        c.wait()
    x_local.wait()
    for t in range(tiles - 2, tiles):
        own_copy(t).wait()
    for t in range(tiles - KEEP, tiles):
        for c in s2_copies(t):
            c.wait()
    for t in range(tiles - SENDS, tiles):
        for k in (0, 1):
            t_hop(t, k, True).wait_send()

    def finish_dy(j, _):
        for kind in range(4):
            hop(kind, j, True).wait_send()
        return 0

    lax.fori_loop(0, blocks, finish_dy, 0)

    def finish_first(c, _):
        xhop(1, c, False).wait_recv()
        xhop(2, c, False).wait_recv()
        xhop(2, c, True).wait_send()
        for kind in (0, 1):
            xhop(kind, c, True).wait_send()
        return 0

    def finish_second(c, _):
        xhop(0, c, False).wait_recv()
        xhop(3, c, False).wait_recv()
        xhop(3, c, True).wait_send()
        for kind in (0, 1):
            xhop(kind, c, True).wait_send()
        return 0

    lax.fori_loop(0, chunks // 2, finish_first, 0)
    lax.fori_loop(chunks // 2, chunks, finish_second, 0)


def dw_kernel(xf, dg, du, ready, dwg, dwu, copied):
    t = xf[...]
    dwg[...] = dot_tn(t, dg[...]).astype(BF16)
    dwu[...] = dot_tn(t, du[...]).astype(BF16)
    copied[...] = ready[...]


def cost(flops, nbytes):
    return pl.CostEstimate(flops=flops, bytes_accessed=nbytes, transcendentals=0)


def solution(mesh):
    n = mesh.shape["tp"]

    def body(x, dy, gate, up, w_gate, w_up, w_down):
        share, width = x.shape
        rows, ff = gate.shape
        blocks, tiles, half = width // CB, width // NT, share // 2
        any_, vmem, dma = pl.BlockSpec(memory_space=pl.ANY), pltpu.VMEM, pltpu.SemaphoreType.DMA
        flops = 2 * rows * width * ff
        act, wbytes = rows * ff * 2, width * ff * 2
        shape = jax.ShapeDtypeStruct

        dg, du, dwd, xf, to_r, to_l, own = pl.pallas_call(
            functools.partial(main_kernel, n),
            out_shape=[
                shape((rows, ff), BF16),
                shape((rows, ff), BF16),
                shape((ff, width), BF16),
                shape((rows, width), BF16),
                shape((share, width), BF16),
                shape((share, width), BF16),
                shape((share, width), F32),
            ],
            in_specs=[any_] * 7,
            out_specs=[any_] * 7,
            scratch_shapes=[
                vmem((blocks, rows, CB), BF16),
                vmem((ff, rows), BF16),
                vmem((ff // ET, rows, ET), F32),
                vmem((rows, ff), BF16),
                vmem((rows, ff), BF16),
                vmem((2, FT, CB), BF16),
                vmem((2, FT, CB), BF16),
                vmem((2, 2, rows, ET), BF16),
                vmem((2, 2, NT, ff), BF16),
                vmem((SENDS, 2, half, NT), BF16),
                vmem((tiles, 2, half, NT), BF16),
                dma((blocks,)),
                dma((4, blocks)),
                dma((4, blocks)),
                dma((2,)),
                dma((2,)),
                dma((2, 2)),
                dma((3,)),
                dma((2, 2)),
                dma((4, share // XR)),
                dma((4, share // XR)),
                dma((SENDS, 2)),
                dma((tiles, 2)),
                dma((KEEP, 2)),
                dma((2,)),
            ],
            compiler_params=pltpu.CompilerParams(collective_id=0, has_side_effects=True, vmem_limit_bytes=VMEM_LIMIT),
            cost_estimate=cost(4 * flops, 4 * wbytes + 8 * act),
            name="dhidden_dwdown_dx",
        )(dy, gate, up, w_down, w_gate, w_up, x)

        from_l = lax.ppermute(to_r, "tp", [(i, (i + 1) % n) for i in range(n)])
        from_r = lax.ppermute(to_l, "tp", [(i, (i - 1) % n) for i in range(n)])

        whole = pl.BlockSpec((rows, ff), lambda i: (0, 0), pipeline_mode=pl.Buffered(1))
        out_spec = pl.BlockSpec((DT, ff), lambda i: (i, 0))
        copy_spec = pl.BlockSpec((ff * DT // width, width), lambda i: (i, 0))
        dwg, dwu, dwd = pl.pallas_call(
            dw_kernel,
            grid=(width // DT,),
            out_shape=[shape((width, ff), BF16), shape((width, ff), BF16), shape((ff, width), BF16)],
            in_specs=[pl.BlockSpec((rows, DT), lambda i: (0, i)), whole, whole, copy_spec],
            out_specs=[out_spec, out_spec, copy_spec],
            compiler_params=pltpu.CompilerParams(vmem_limit_bytes=VMEM_LIMIT, dimension_semantics=("arbitrary",)),
            cost_estimate=cost(2 * flops, 4 * wbytes + 4 * act),
            name="dw_gate_up",
        )(xf, dg, du, dwd)

        dx = (own + from_l.astype(F32) + from_r.astype(F32)).astype(BF16)
        return dx, dwg, dwu, dwd

    part, cols = P(("dp", "tp"), None), P("dp", "tp")
    return jax.shard_map(
        body,
        mesh=mesh,
        in_specs=(part, part, cols, cols, P(None, "tp"), P(None, "tp"), P("tp", None)),
        out_specs=(part, cols, cols, part),
        check_vma=False,
    )
```

time: 350 us -> 320 us (0.914)
  Pallas kernels: 324 us -> 309 us
  local copies, waits for them, and re-layouts: 7.97 us -> 0 us
  other arithmetic: 10.5 us -> 6.15 us
    pallas_call x4 -> x2, Pallas kernels: 324 us -> 309 us  [the longest x1 217 us: body(): pl.pallas_call(functools.partial(main_kernel, n), out_shape=[shape((rows,...]
    slice x6 -> x0, local copies, waits for them, and re-layouts: 7.11 us -> none  [the longest x2 2.7 us: body(): first = f32(jnp.concatenate([r2r[:half], r2l[:half]]))]
    convert_element_type x3 -> x1, other arithmetic: 7.77 us -> 6.15 us  [body(): dx = (own + from_l.astype(F32) + from_r.astype(F32)).astype(BF16)]
  transfers between devices with their start and end apart: 4 -> 2, of which waited for: 0 -> 0; matrix products, arithmetic and copies ran while one was open for 3% -> 0% of each run, Pallas kernels for 32% -> 29%
where the time goes in v2:
time: 320 us; the launch traced here: 319 us
  Pallas kernels  309 us (97%)
  other arithmetic  6.15 us (2%)
  starting transfers between devices  3.31 us (1%)
    pallas_call x1, Pallas kernels, body(): pl.pallas_call(functools.partial(main_kernel, n), out_shape=[shape((rows,...  217 us
    pallas_call x1, Pallas kernels, body(): pl.pallas_call(dw_kernel, grid=(width // DT,), out_shape=[shape((width, f...  92.3 us
  transfers between devices with their start and end apart: 2, of which 0 were waited for; matrix products, arithmetic and copies ran while one was open for 0% of the time, Pallas kernels for 29%

profile of v2, /device:TPU:112, one launch (start us, length us, event | category | flops | bytes accessed | tf_op | source)
XLA Modules:
  0.0 319.3 jit_solution(6403909405541746410)
XLA Ops:
  0.6 216.9 %dhidden_dwdown_dx.1 = (bf16[768,4096]{1,0:T(8,128)(2,1)}, bf16[768,4096]{1,0:T(8,128)(2,1)}, bf16[4096,6144]{1,0:T(8,128)(2,1)}, bf16[768,6144]{1,0:T(8,128)(2,...) custom-call(bf16[192,6144]{1,0:T(8,128)(2,1)} %dy.1, bf16[768,4096]{1,0:T(8,128)(2,1)} %gate.1, ...), custom_call_target="tpu_custom_call" | custom-call | flops 154618822656 | bytes 251658240 | tf_op jit(solution)/shard_map/dhidden_dwdown_dx/pallas_call | solution.py:410
  217.5 0.1 collective-permute-start
  217.6 3.2 %collective-permute-start.1 = (bf16[192,6144]{1,0:T(8,128)(2,1)}, bf16[192,6144]{1,0:T(8,128)(2,1)}, u32[]{:S(2)}, u32[]{:S(2)}) collective-permute-start(bf16[192,6144]{1,0:T(8,128)(2,1)} %get-tuple-element.16), channel_id=1, source_target_pairs={{0,3},{1,0},{2,1},{3,2},{4,7},{5,4},{6,5},{7,6},{8,11},{9,8},{10,9... | collective-permute-start | bytes 7077896 | tf_op jit(solution)/shard_map/ppermute | solution.py:456
  220.8 92.3 %dw_gate_up.1 = (bf16[6144,4096]{1,0:T(8,128)(2,1)}, bf16[6144,4096]{1,0:T(8,128)(2,1)}, bf16[4096,6144]{1,0:T(8,128)(2,1)}) custom-call(bf16[768,6144]{1,0:T(8,128)(2,1)} %get-tuple-element.17.xf, bf16[768,4096]{1,0:T(8,128)(2,1)} %get-tuple-element.18.dg, bf16[768,4096]{1,0:T(8,128)(2,1)} %get-tuple-element.19.du, bf16[4096,6144]{1,0:T(8,128)(2,1)} %get-tuple-element.20.ready), custom_call_target="tpu_custom_call" | custom-call | flops 77309411328 | bytes 226492416 | tf_op jit(solution)/shard_map/dw_gate_up/pallas_call | solution.py:461
  313.1 0.0 collective-permute-done
  313.1 0.0 collective-permute-done.1
  313.1 6.1 %add_convert_fusion = bf16[192,6144]{1,0:T(8,128)(2,1)} fusion(bf16[192,6144]{1,0:T(8,128)(2,1)} %collective-permute-done.1, f32[192,6144]{1,0:T(8,128)} %get-tuple-element.14, bf16[192,6144]{1,0:T(8,128)(2,1)} %collective-permute-done), kind=kLoop, calls=%fused_computation | loop fusion | flops 5898240 | bytes 11796480 | tf_op jit(solution)/shard_map/convert_element_type | solution.py:472
Async XLA Ops:
  217.5 95.6 %collective-permute-start = (bf16[192,6144]{1,0:T(8,128)(2,1)}, bf16[192,6144]{1,0:T(8,128)(2,1)}, u32[]{:S(2)}, u32[]{:S(2)}) collective-permute-start(bf16[192,6144]{1,0:T(8,128)(2,1)} %get-tuple-element.15), channel_id=1, source_target_pairs={{0,1},{1,2},{2,3},{3,0},{4,5},{5,6},{6,7},{7,4},{8,9},{9,10},{10,1... | collective-permute-start | bytes 7077896 | tf_op jit(solution)/shard_map/ppermute | solution.py:455
  217.6 95.5 %collective-permute-start.1 = (bf16[192,6144]{1,0:T(8,128)(2,1)}, bf16[192,6144]{1,0:T(8,128)(2,1)}, u32[]{:S(2)}, u32[]{:S(2)}) collective-permute-start(bf16[192,6144]{1,0:T(8,128)(2,1)} %get-tuple-element.16), channel_id=1, source_target_pairs={{0,3},{1,0},{2,1},{3,2},{4,7},{5,4},{6,5},{7,6},{8,11},{9,8},{10,9... | collective-permute-start | bytes 7077896 | tf_op jit(solution)/shard_map/ppermute | solution.py:456

commit v3 on v2

--- a/solution.py
+++ b/solution.py
@@ -12,13 +12,13 @@
 VMEM_LIMIT = 66_000_000
 
 CB = 512
-FT = 1024
+FT = 2048
 ET = 512
 NT = 256
 DT = 384
 XR = 16
-DELAY = 4
-KEEP = DELAY + 2
+DELAY = 5
+KEEP = DELAY + 1
 SENDS = 4
 
 
@@ -56,7 +56,7 @@
     n,
     dy, gate, up, wd, wg, wu, x,
     dg, du, dwd, xf, to_r, to_l, own,
-    dyf, hid_t, acc, dgv, duv, wbuf, obuf, gu, w2, rsend, rrecv,
+    dyf, hid_t, acc, dgv, duv, wbuf, gu, w2, rsend, rrecv,
     lsem, ssem, rsem, wsem, osem, gsem, dsem, w2sem, xsend, xrecv, ts, tr, s2sem, owsem,
 ):
     me, right, left, opposite = ring(n)
@@ -74,24 +74,21 @@
 
     def hop(kind, j, sending):
         to = right if kind % 2 == 0 else left
-        if kind < 2:
-            start, size = 0, share
-            whose = me if sending else (left if kind == 0 else right)
+        if kind < 4:
+            whose = me if sending else (left if kind % 2 == 0 else right)
         else:
-            start, size = (0 if kind == 2 else half), half
-            whose = (left if kind == 2 else right) if sending else opposite
-        part = dyf.at[j, rows_of(whose, share, start, size), :]
+            whose = (left if kind == 4 else right) if sending else opposite
+        part = dyf.at[j, rows_of(whose, share, half if kind in (1, 2, 5) else 0, half), :]
         return remote(part, part, ssem.at[kind, j], rsem.at[kind, j], to)
 
     def send_own(j):
-        hop(0, j, True).start()
-        hop(1, j, True).start()
+        for kind in range(4):
+            hop(kind, j, True).start()
 
     def pass_on(j):
         for kind in (0, 1):
             hop(kind, j, False).wait_recv()
-        hop(2, j, True).start()
-        hop(3, j, True).start()
+            hop(kind + 4, j, True).start()
 
     def gu_copies(e, slot):
         cols = pl.ds(pl.multiple_of(e * et, et), et)
@@ -103,8 +100,20 @@
     def w_copy(s):
         return pltpu.make_async_copy(tile(wd, s // steps_f, lax.rem(s, steps_f)), wbuf.at[lax.rem(s, 2)], wsem.at[lax.rem(s, 2)])
 
-    def o_copy(s):
-        return pltpu.make_async_copy(obuf.at[lax.rem(s, 2)], tile(dwd, s // steps_f, lax.rem(s, steps_f)), osem.at[lax.rem(s, 2)])
+    nt = w2.shape[2]
+    panels = ft // nt
+
+    def panel(slot, q):
+        return w2.at[1, slot, :, q * cb : (q + 1) * cb]
+
+    def o_copies(s):
+        slot = lax.rem(s, 2)
+        cols = pl.ds(pl.multiple_of(s // steps_f * cb, cb), cb)
+        start = lax.rem(s, steps_f) * ft
+        return [
+            pltpu.make_async_copy(panel(slot, q), dwd.at[pl.ds(pl.multiple_of(start + q * nt, nt), nt), cols], osem.at[slot, q])
+            for q in range(panels)
+        ]
 
     chunks = share // XR
 
@@ -138,8 +147,8 @@
     greet(right, left)
     for j in range(blocks):
         load(j).wait()
-        if j < 2:
-            send_own(j)
+        if j == 0:
+            send_own(0)
 
     def hidden_step(e, _):
         slot = lax.rem(e, 2)
@@ -158,10 +167,11 @@
         acc[e] = jnp.zeros(acc.shape[1:], F32)
         return 0
 
-    lax.fori_loop(0, tiles_e // 2, hidden_step, 0)
+    lax.fori_loop(0, tiles_e * 3 // 8, hidden_step, 0)
     pass_on(0)
+    send_own(1)
     send_own(2)
-    lax.fori_loop(tiles_e // 2, tiles_e, hidden_step, 0)
+    lax.fori_loop(tiles_e * 3 // 8, tiles_e, hidden_step, 0)
 
     total = blocks * steps_f
 
@@ -172,7 +182,7 @@
 
         @pl.when(f == 0)
         def _():
-            for kind in (2, 3):
+            for kind in (2, 3, 4, 5):
                 hop(kind, j, False).wait_recv()
 
             @pl.when(j + 1 < blocks)
@@ -195,13 +205,17 @@
 
         @pl.when(s >= 2)
         def _():
-            o_copy(s - 2).wait()
+            for c in o_copies(s - 2):
+                c.wait()
 
         block = dyf[j]
         for q in range(per_step):
             acc[f * per_step + q] += dot_nt(block, wbuf[slot, q * et : (q + 1) * et, :])
-        obuf[slot] = jnp.dot(hid_t[pl.ds(pl.multiple_of(f * ft, ft), ft), :], block, preferred_element_type=F32).astype(BF16)
-        o_copy(s).start()
+        product = jnp.dot(hid_t[pl.ds(pl.multiple_of(f * ft, ft), ft), :], block, preferred_element_type=F32).astype(BF16)
+        for q in range(panels):
+            panel(slot, q)[...] = product[q * nt : (q + 1) * nt]
+        for c in o_copies(s):
+            c.start()
         return 0
 
     for c in gu_copies(0, 0):
@@ -209,15 +223,15 @@
     lax.fori_loop(0, total, step, 0)
 
     width = wg.shape[0]
-    nt = w2.shape[2]
     tiles = width // nt
-    res = acc.at[0, :, :nt]
+    def res(slot):
+        return acc.at[slot, :, :nt]
 
     def keep(hold, k):
-        return acc.at[1 + hold, k * half : (k + 1) * half, :nt]
+        return acc.at[2 + hold, k * half : (k + 1) * half, :nt]
 
     def sto(slot):
-        return acc.at[1 + KEEP, pl.ds(pl.multiple_of(slot * share, 16), share), :nt]
+        return acc.at[0, pl.ds(pl.multiple_of(slot * share, 16), share), nt : 2 * nt]
 
     def st2(hold, k, start, size):
         return gu.at[hold // 4, k, pl.ds(pl.multiple_of(lax.rem(hold, 4) * share + start, 16), size), :nt]
@@ -273,11 +287,51 @@
         slot = lax.rem(t, 2)
         return pltpu.make_async_copy(sto(slot), own.at[:, pl.ds(pl.multiple_of(t * nt, nt), nt)], owsem.at[slot])
 
+    def free_slots(p):
+        @pl.when(p >= SENDS)
+        def _():
+            for k in (0, 1):
+                t_hop(p - SENDS, k, True).wait_send()
+
+        @pl.when(p >= KEEP)
+        def _():
+            for c in s2_copies(p - KEEP):
+                c.wait()
+
+        @pl.when(p >= 2)
+        def _():
+            own_copy(p - 2).wait()
+
+    def strips(slot, hold, out):
+        def term(device, start, size):
+            return res(slot)[rows_of(device, share, start, size), :]
+
+        rsend[out, 0] = term(opposite, 0, half).astype(BF16)
+        rsend[out, 1] = term(opposite, half, half).astype(BF16)
+        keep(hold, 0)[...] = term(right, 0, half)
+        keep(hold, 1)[...] = term(left, half, half)
+        st2(hold, 0, half, half)[...] = term(right, half, half).astype(BF16)
+        st2(hold, 1, 0, half)[...] = term(left, 0, half).astype(BF16)
+        sto(slot)[...] = term(me, 0, share)
+
+    def arrive(u):
+        hold = lax.rem(u, KEEP)
+        for k in (0, 1):
+            t_hop(u, k, False).wait_recv()
+        st2(hold, 0, 0, half)[...] = (keep(hold, 0)[...] + rrecv[u, 0].astype(F32)).astype(BF16)
+        st2(hold, 1, half, half)[...] = (keep(hold, 1)[...] + rrecv[u, 1].astype(F32)).astype(BF16)
+        for c in s2_copies(u):
+            c.start()
+
+    for s in (total - 2, total - 1):
+        for c in o_copies(s):
+            c.wait()
+
     def dx_step(t, _):
-        @pl.when(jnp.logical_and(t >= 1, t <= tiles))
+        @pl.when(t >= 2)
         def _():
             for k in (0, 1):
-                t_hop(t - 1, k, True).start()
+                t_hop(t - 2, k, True).start()
 
         @pl.when(jnp.logical_and(lax.rem(t, 4) == 0, t < 2 * chunks))
         def _():
@@ -287,64 +341,44 @@
         def _():
             x_own(chunks // 2 + t // 4)
 
-        @pl.when(t < tiles)
-        def _():
-            slot = lax.rem(t, 2)
-            for c in w2_copies(t):
-                c.wait()
-
-            @pl.when(t + 1 < tiles)
-            def _():
-                for c in w2_copies(t + 1):
-                    c.start()
-
-            @pl.when(t >= SENDS)
-            def _():
-                for k in (0, 1):
-                    t_hop(t - SENDS, k, True).wait_send()
-
-            @pl.when(t >= KEEP)
-            def _():
-                for c in s2_copies(t - KEEP):
-                    c.wait()
-
-            @pl.when(t >= 2)
-            def _():
-                own_copy(t - 2).wait()
-
-            res[...] = dot_nt(dgv[...], w2[slot, 0]) + dot_nt(duv[...], w2[slot, 1])
-
-            def term(device, start, size):
-                return res[rows_of(device, share, start, size), :]
-
-            hold = lax.rem(t, KEEP)
-            out = lax.rem(t, SENDS)
-            rsend[out, 0] = term(opposite, 0, half).astype(BF16)
-            rsend[out, 1] = term(opposite, half, half).astype(BF16)
-            keep(hold, 0)[...] = term(right, 0, half)
-            keep(hold, 1)[...] = term(left, half, half)
-            st2(hold, 0, half, half)[...] = term(right, half, half).astype(BF16)
-            st2(hold, 1, 0, half)[...] = term(left, 0, half).astype(BF16)
-            sto(slot)[...] = term(me, 0, share)
-            own_copy(t).start()
-
         @pl.when(t >= DELAY)
         def _():
-            u = t - DELAY
-            hold = lax.rem(u, KEEP)
-            for k in (0, 1):
-                t_hop(u, k, False).wait_recv()
-            st2(hold, 0, 0, half)[...] = (keep(hold, 0)[...] + rrecv[u, 0].astype(F32)).astype(BF16)
-            st2(hold, 1, half, half)[...] = (keep(hold, 1)[...] + rrecv[u, 1].astype(F32)).astype(BF16)
-            for c in s2_copies(u):
+            arrive(t - DELAY)
+
+        slot = lax.rem(t, 2)
+        for c in w2_copies(t):
+            c.wait()
+
+        @pl.when(t + 1 < tiles)
+        def _():
+            for c in w2_copies(t + 1):
                 c.start()
 
-        return 0
-
-    lax.fori_loop(0, tiles + DELAY, dx_step, 0)
-
-    for s in (total - 2, total - 1):
-        o_copy(s).wait()
+        free_slots(t - 1)
+        res(slot)[...] = dot_nt(dgv[...], w2[slot, 0]) + dot_nt(duv[...], w2[slot, 1])
+        strips(1 - slot, lax.rem(t + KEEP - 1, KEEP), lax.rem(t + SENDS - 1, SENDS))
+
+        @pl.when(t >= 1)
+        def _():
+            own_copy(t - 1).start()
+
+        return 0
+
+    lax.fori_loop(0, tiles, dx_step, 0)
+    last = tiles - 1
+    for k in (0, 1):
+        t_hop(last - 1, k, True).start()
+    free_slots(last)
+    strips(last % 2, last % KEEP, last % SENDS)
+    own_copy(last).start()
+    for k in (0, 1):
+        t_hop(last, k, True).start()
+
+    def late(u, _):
+        arrive(u)
+        return 0
+
+    lax.fori_loop(tiles - DELAY, tiles, late, 0)
     for c in d_copies:
         c.wait()
     x_local.wait()
@@ -358,7 +392,7 @@
             t_hop(t, k, True).wait_send()
 
     def finish_dy(j, _):
-        for kind in range(4):
+        for kind in range(6):
             hop(kind, j, True).wait_send()
         return 0
 
@@ -384,11 +418,40 @@
     lax.fori_loop(chunks // 2, chunks, finish_second, 0)
 
 
-def dw_kernel(xf, dg, du, ready, dwg, dwu, copied):
+def dw_kernel(xf, dg, du, ready, dwg, dwu, copied, cbuf, isem, osem):
+    i = pl.program_id(0)
+    steps = pl.num_programs(0)
+    size = cbuf.shape[1]
+
+    def copies(c):
+        slot = lax.rem(c, 2)
+        part = pl.ds(pl.multiple_of(c * size, size), size)
+        return (
+            pltpu.make_async_copy(ready.at[part, :], cbuf.at[slot], isem.at[slot]),
+            pltpu.make_async_copy(cbuf.at[slot], copied.at[part, :], osem.at[slot]),
+        )
+
+    @pl.when(lax.rem(i, 2) == 0)
+    def _():
+        @pl.when(i >= 4)
+        def _():
+            copies(i // 2 - 2)[1].wait()
+
+        copies(i // 2)[0].start()
+
+    @pl.when(lax.rem(i, 2) == 1)
+    def _():
+        copies(i // 2)[0].wait()
+        copies(i // 2)[1].start()
+
     t = xf[...]
     dwg[...] = dot_tn(t, dg[...]).astype(BF16)
     dwu[...] = dot_tn(t, du[...]).astype(BF16)
-    copied[...] = ready[...]
+
+    @pl.when(i == steps - 1)
+    def _():
+        copies(steps // 2 - 2)[1].wait()
+        copies(steps // 2 - 1)[1].wait()
 
 
 def cost(flops, nbytes):
@@ -427,16 +490,15 @@
                 vmem((rows, ff), BF16),
                 vmem((rows, ff), BF16),
                 vmem((2, FT, CB), BF16),
-                vmem((2, FT, CB), BF16),
                 vmem((2, 2, rows, ET), BF16),
                 vmem((2, 2, NT, ff), BF16),
                 vmem((SENDS, 2, half, NT), BF16),
                 vmem((tiles, 2, half, NT), BF16),
                 dma((blocks,)),
-                dma((4, blocks)),
-                dma((4, blocks)),
+                dma((6, blocks)),
+                dma((6, blocks)),
                 dma((2,)),
-                dma((2,)),
+                dma((2, FT // NT)),
                 dma((2, 2)),
                 dma((3,)),
                 dma((2, 2)),
@@ -457,14 +519,14 @@
 
         whole = pl.BlockSpec((rows, ff), lambda i: (0, 0), pipeline_mode=pl.Buffered(1))
         out_spec = pl.BlockSpec((DT, ff), lambda i: (i, 0))
-        copy_spec = pl.BlockSpec((ff * DT // width, width), lambda i: (i, 0))
         dwg, dwu, dwd = pl.pallas_call(
             dw_kernel,
             grid=(width // DT,),
             out_shape=[shape((width, ff), BF16), shape((width, ff), BF16), shape((ff, width), BF16)],
-            in_specs=[pl.BlockSpec((rows, DT), lambda i: (0, i)), whole, whole, copy_spec],
-            out_specs=[out_spec, out_spec, copy_spec],
-            compiler_params=pltpu.CompilerParams(vmem_limit_bytes=VMEM_LIMIT, dimension_semantics=("arbitrary",)),
+            in_specs=[pl.BlockSpec((rows, DT), lambda i: (0, i)), whole, whole, any_],
+            out_specs=[out_spec, out_spec, any_],
+            scratch_shapes=[vmem((2, ff * DT * 2 // width, width), BF16), dma((2,)), dma((2,))],
+            compiler_params=pltpu.CompilerParams(vmem_limit_bytes=50_000_000, dimension_semantics=("arbitrary",)),
             cost_estimate=cost(2 * flops, 4 * wbytes + 4 * act),
             name="dw_gate_up",
         )(xf, dg, du, dwd)

time: 320 us -> 311 us (0.972)
  Pallas kernels: 309 us -> 301 us
  other arithmetic: 6.15 us -> 2.38 us
    pallas_call x1, Pallas kernels: 92.3 us -> 88.4 us  [body(): pl.pallas_call(dw_kernel, grid=(width // DT,), out_shape=[shape((width, f...]
    pallas_call x1, Pallas kernels: 217 us -> 213 us  [body(): pl.pallas_call(functools.partial(main_kernel, n), out_shape=[shape((rows,...]
    convert_element_type x1, other arithmetic: 6.15 us -> 2.38 us  [body(): dx = (own + from_l.astype(F32) + from_r.astype(F32)).astype(BF16)]
  transfers between devices with their start and end apart: 2 -> 2, of which waited for: 0 -> 0; matrix products, arithmetic and copies ran while one was open for 0% -> 0% of each run, Pallas kernels for 29% -> 28%
where the time goes in v3:
time: 311 us
  Pallas kernels  301 us (97%)
  starting transfers between devices  3.31 us (1%)
    pallas_call x1, Pallas kernels, body(): pl.pallas_call(functools.partial(main_kernel, n), out_shape=[shape((rows,...  213 us
    pallas_call x1, Pallas kernels, body(): pl.pallas_call(dw_kernel, grid=(width // DT,), out_shape=[shape((width, f...  88.4 us
  transfers between devices with their start and end apart: 2, of which 0 were waited for; matrix products, arithmetic and copies ran while one was open for 0% of the time, Pallas kernels for 28%

profile of v3, /device:TPU:112, one launch (start us, length us, event | category | flops | bytes accessed | tf_op | source)
XLA Modules:
  0.0 310.6 jit_solution(15263047947934269332)
XLA Ops:
  0.6 213.1 %dhidden_dwdown_dx.1 = (bf16[768,4096]{1,0:T(8,128)(2,1)}, bf16[768,4096]{1,0:T(8,128)(2,1)}, bf16[4096,6144]{1,0:T(8,128)(2,1)}, bf16[768,6144]{1,0:T(8,128)(2,...) custom-call(bf16[192,6144]{1,0:T(8,128)(2,1)} %dy.1, bf16[768,4096]{1,0:T(8,128)(2,1)} %gate.1, ...), custom_call_target="tpu_custom_call" | custom-call | flops 154618822656 | bytes 251658240 | tf_op jit(solution)/shard_map/dhidden_dwdown_dx/pallas_call | solution.py:473
  213.7 0.6 collective-permute-start
  214.3 2.7 collective-permute-start.1
  217.0 0.0 copy-start
  217.0 2.8 copy-done
  219.8 0.0 copy-start.1
  219.8 88.4 %dw_gate_up.1 = (bf16[6144,4096]{1,0:T(8,128)(2,1)}, bf16[6144,4096]{1,0:T(8,128)(2,1)}, bf16[4096,6144]{1,0:T(8,128)(2,1)}) custom-call(bf16[768,6144]{1,0:T(8,128)(2,1)} %get-tuple-element.17.xf, bf16[768,4096]{1,0:T(8,128)(2,1)S(1)} %copy-done, bf16[768,4096]{1,0:T(8,128)(2,1)} %get-tuple-element.19.du, bf16[4096,6144]{1,0:T(8,128)(2,1)} %get-tuple-element.20.ready), custom_call_target="tpu_custom_call" | custom-call | flops 77309411328 | bytes 226492416 | tf_op jit(solution)/shard_map/dw_gate_up/pallas_call | solution.py:522
  308.2 0.0 collective-permute-done
  308.2 0.0 collective-permute-done.1
  308.3 0.0 copy-done.1
  308.3 2.4 add_convert_fusion
Async XLA Ops:
  213.7 94.5 %collective-permute-start = (bf16[192,6144]{1,0:T(8,128)(2,1)}, bf16[192,6144]{1,0:T(8,128)(2,1)S(1)}, u32[]{:S(2)}, u32[]{:S(2)}) collective-permute-start(bf16[192,6144]{1,0:T(8,128)(2,1)} %get-tuple-element.15), channel_id=1, source_target_pairs={{0,1},{1,2},{2,3},{3,0},{4,5},{5,6},{6,7},{7,4},{8,9},{9,10},{10,1... | collective-permute-start | bytes 7077896 | tf_op jit(solution)/shard_map/ppermute | solution.py:517
  214.3 93.9 %collective-permute-start.1 = (bf16[192,6144]{1,0:T(8,128)(2,1)}, bf16[192,6144]{1,0:T(8,128)(2,1)S(1)}, u32[]{:S(2)}, u32[]{:S(2)}) collective-permute-start(bf16[192,6144]{1,0:T(8,128)(2,1)} %get-tuple-element.16), channel_id=1, source_target_pairs={{0,3},{1,0},{2,1},{3,2},{4,7},{5,4},{6,5},{7,6},{8,11},{9,8},{10,9... | collective-permute-start | bytes 7077896 | tf_op jit(solution)/shard_map/ppermute | solution.py:518
  217.0 2.8 copy-start
  219.8 88.4 %copy-start.1 = (f32[192,6144]{1,0:T(8,128)S(1)}, f32[192,6144]{1,0:T(8,128)}, u32[]{:S(2)}) copy-start(f32[192,6144]{1,0:T(8,128)} %get-tuple-element.14) | copy-start | bytes 14155780

commit v4 on v3

--- a/solution.py
+++ b/solution.py
@@ -526,7 +526,7 @@
             in_specs=[pl.BlockSpec((rows, DT), lambda i: (0, i)), whole, whole, any_],
             out_specs=[out_spec, out_spec, any_],
             scratch_shapes=[vmem((2, ff * DT * 2 // width, width), BF16), dma((2,)), dma((2,))],
-            compiler_params=pltpu.CompilerParams(vmem_limit_bytes=50_000_000, dimension_semantics=("arbitrary",)),
+            compiler_params=pltpu.CompilerParams(vmem_limit_bytes=55_000_000, dimension_semantics=("arbitrary",)),
             cost_estimate=cost(2 * flops, 4 * wbytes + 4 * act),
             name="dw_gate_up",
         )(xf, dg, du, dwd)

time: 311 us -> 310 us (level)
  transfers between devices with their start and end apart: 2 -> 2, of which waited for: 0 -> 0; matrix products, arithmetic and copies ran while one was open for 0% -> 0% of each run, Pallas kernels for 28% -> 29%
where the time goes in v4:
time: 310 us
  Pallas kernels  303 us (98%)
  starting transfers between devices  3.31 us (1%)
    pallas_call x1, Pallas kernels, body(): pl.pallas_call(functools.partial(main_kernel, n), out_shape=[shape((rows,...  213 us
    pallas_call x1, Pallas kernels, body(): pl.pallas_call(dw_kernel, grid=(width // DT,), out_shape=[shape((width, f...  90.2 us
  transfers between devices with their start and end apart: 2, of which 0 were waited for; matrix products, arithmetic and copies ran while one was open for 0% of the time, Pallas kernels for 29%

profile of v4, /device:TPU:112, one launch (start us, length us, event | category | flops | bytes accessed | tf_op | source)
XLA Modules:
  0.0 309.6 jit_solution(3504903736488073599)
XLA Ops:
  0.6 213.1 %dhidden_dwdown_dx.1 = (bf16[768,4096]{1,0:T(8,128)(2,1)}, bf16[768,4096]{1,0:T(8,128)(2,1)}, bf16[4096,6144]{1,0:T(8,128)(2,1)}, bf16[768,6144]{1,0:T(8,128)(2,...) custom-call(bf16[192,6144]{1,0:T(8,128)(2,1)} %dy.1, bf16[768,4096]{1,0:T(8,128)(2,1)} %gate.1, ...), custom_call_target="tpu_custom_call" | custom-call | flops 154618822656 | bytes 251658240 | tf_op jit(solution)/shard_map/dhidden_dwdown_dx/pallas_call | solution.py:473
  213.7 0.6 collective-permute-start
  214.3 2.7 collective-permute-start.1
  217.0 0.0 copy-start
  217.0 90.2 %dw_gate_up.1 = (bf16[6144,4096]{1,0:T(8,128)(2,1)}, bf16[6144,4096]{1,0:T(8,128)(2,1)}, bf16[4096,6144]{1,0:T(8,128)(2,1)}) custom-call(bf16[768,6144]{1,0:T(8,128)(2,1)} %get-tuple-element.17.xf, bf16[768,4096]{1,0:T(8,128)(2,1)} %get-tuple-element.18.dg, bf16[768,4096]{1,0:T(8,128)(2,1)} %get-tuple-element.19.du, bf16[4096,6144]{1,0:T(8,128)(2,1)} %get-tuple-element.20.ready), custom_call_target="tpu_custom_call" | custom-call | flops 77309411328 | bytes 226492416 | tf_op jit(solution)/shard_map/dw_gate_up/pallas_call | solution.py:522
  307.2 0.0 collective-permute-done
  307.2 0.0 collective-permute-done.1
  307.2 0.0 copy-done
  307.2 2.4 add_convert_fusion
Async XLA Ops:
  213.7 93.5 %collective-permute-start = (bf16[192,6144]{1,0:T(8,128)(2,1)}, bf16[192,6144]{1,0:T(8,128)(2,1)S(1)}, u32[]{:S(2)}, u32[]{:S(2)}) collective-permute-start(bf16[192,6144]{1,0:T(8,128)(2,1)} %get-tuple-element.15), channel_id=1, source_target_pairs={{0,1},{1,2},{2,3},{3,0},{4,5},{5,6},{6,7},{7,4},{8,9},{9,10},{10,1... | collective-permute-start | bytes 7077896 | tf_op jit(solution)/shard_map/ppermute | solution.py:517
  214.3 92.9 %collective-permute-start.1 = (bf16[192,6144]{1,0:T(8,128)(2,1)}, bf16[192,6144]{1,0:T(8,128)(2,1)S(1)}, u32[]{:S(2)}, u32[]{:S(2)}) collective-permute-start(bf16[192,6144]{1,0:T(8,128)(2,1)} %get-tuple-element.16), channel_id=1, source_target_pairs={{0,3},{1,0},{2,1},{3,2},{4,7},{5,4},{6,5},{7,6},{8,11},{9,8},{10,9... | collective-permute-start | bytes 7077896 | tf_op jit(solution)/shard_map/ppermute | solution.py:518
  217.0 90.2 %copy-start = (f32[192,6144]{1,0:T(8,128)S(1)}, f32[192,6144]{1,0:T(8,128)}, u32[]{:S(2)}) copy-start(f32[192,6144]{1,0:T(8,128)} %get-tuple-element.14) | copy-start | bytes 14155780
